TPU v7x, 32 devices: a whole 2x2x4 slice. The times are simulated.
32 devices in a mesh: width: 8 (over z, core), lat: 4 (over y, x).
Axes of the slice: x: 2, y: 2, z: 4, core: 2. Of those that a mesh axis runs over, the one named last changes fastest.
Arguments:
- residuals: bfloat16 [384, 16384], P(None, 'width'), may hold values from -6 to 6
- encoder: bfloat16 [16384, 4096], P('width', 'lat'), may hold values from -0.046875 to 0.046875
- enc_bias: float32 [4096], P('lat'), may hold values from -3 to 3
- decoder: bfloat16 [4096, 16384], P('lat', 'width'), may hold values from -0.046875 to 0.046875
- dec_bias: float32 [16384], P('width'), may hold values from -3 to 3
Outputs:
- enc_grad: bfloat16 [16384, 4096], P('width', 'lat')
- new_decoder: bfloat16 [4096, 16384], P('lat', 'width')
All inputs are finite; a program needn't handle non-finite values.
Results may differ from a plain program's by a relative error of at most 0.011.
Values may be sent and summed in bfloat16 or wider, within the bound.
A program may use at most 64 MiB of HBM per device.

v0:
```python
import jax
import jax.numpy as jnp
from jax import lax
from jax.sharding import PartitionSpec as P

EPS = 1e-06
STEP = 0.0003
PENALTY = 0.5


def per_device(residuals, encoder, enc_bias, decoder, dec_bias):
    tokens = residuals.shape[0]
    lat_count = lax.axis_size("lat")
    lat_rows = tokens // lat_count
    rows = residuals
    pre_rows = (
        lax.psum_scatter(
            jnp.dot(rows, encoder, preferred_element_type=jnp.float32),
            "width",
            scatter_dimension=0,
            tiled=True,
        )
        + enc_bias
    )
    active_rows = pre_rows > 0.0
    act_rows = jnp.maximum(pre_rows, 0.0).astype(jnp.bfloat16)
    acts = lax.all_gather(act_rows, "width", axis=0, tiled=True)
    rows = acts
    recon_rows = lax.psum_scatter(
        jnp.dot(rows, decoder, preferred_element_type=jnp.float32),
        "lat",
        scatter_dimension=0,
        tiled=True,
    )
    first = lax.axis_index("lat") * lat_rows
    own_rows = lax.dynamic_slice_in_dim(residuals, first, lat_rows, 0)
    error_part = (recon_rows + dec_bias - own_rows.astype(jnp.float32)).astype(jnp.bfloat16)
    error = lax.all_gather(error_part, "lat", axis=0, tiled=True)
    rows = error
    dacts_rows = (
        lax.psum_scatter(
            lax.dot_general(
                rows, decoder, (((1,), (1,)), ((), ())), preferred_element_type=jnp.float32
            ),
            "width",
            scatter_dimension=0,
            tiled=True,
        )
        + PENALTY
    )
    dpre_part = jnp.where(active_rows, dacts_rows, 0.0).astype(jnp.bfloat16)
    dpre = lax.all_gather(dpre_part, "width", axis=0, tiled=True)
    enc_grad = lax.dot_general(
        residuals, dpre, (((0,), (0,)), ((), ())), preferred_element_type=jnp.float32
    ).astype(jnp.bfloat16)
    grad = lax.dot_general(
        acts, error, (((0,), (0,)), ((), ())), preferred_element_type=jnp.float32
    )
    weight = decoder.astype(jnp.float32)
    ww, gw, gg = lax.psum(
        (
            jnp.sum(weight * weight, axis=1),
            jnp.sum(grad * weight, axis=1),
            jnp.sum(grad * grad, axis=1),
        ),
        "width",
    )
    coef_row = gw / (ww + EPS)
    coef = coef_row[:, None]
    moved = weight - STEP * (grad - coef * weight)
    squared = (
        ww
        - 2.0 * STEP * (gw - coef_row * ww)
        + STEP * STEP * (gg - 2.0 * coef_row * gw + coef_row * coef_row * ww)
    )
    new_decoder = (moved / jnp.sqrt(squared + EPS)[:, None]).astype(jnp.bfloat16)
    return (enc_grad, new_decoder)


def solution(mesh):
    return jax.shard_map(
        per_device,
        mesh=mesh,
        in_specs=(P(None, "width"), P("width", "lat"), P("lat"), P("lat", "width"), P("width")),
        out_specs=(P("width", "lat"), P("lat", "width")),
        check_vma=False,
    )
```

profile of v0, /device:TPU:0, one launch (start us, length us, event | category | flops | bytes accessed | tf_op | source)
XLA Modules:
  0.0 231.2 jit_solution(5187038718343978756)
XLA Ops:
  7.2 0.0 copy-start.2
  7.2 0.0 reduce-scatter.4.cloned.1.call-start
  7.2 5.6 %fusion.6 = f32[384,1024]{1,0:T(8,128)} fusion(bf16[384,2048]{1,0:T(8,128)(2,1)} %param.5, bf16[2048,1024]{1,0:T(8,128)(2,1)} %param.6), kind=kOutput, calls=%fused_computation.17 | convolution fusion | flops 1610612736 | bytes 7340032 | tf_op jit(solution)/shard_map/dot_general | solution.py:18
  12.8 0.0 reduce-scatter.4.cloned.1.call-update
  12.8 0.0 reduce-scatter.6.cloned.1.call-start
  12.9 37.0 %reduce-scatter.4.cloned.1.call-done = f32[48,1024]{1,0:T(8,128)} async-done(((f32[384,1024]{1,0:T(8,128)}), f32[48,1024]{1,0:T(8,128)}) %reduce-scatter.4.cloned.1.call-update) | async-done | bytes 196624 | tf_op jit(solution)/shard_map/reduce_scatter | solution.py:17
  49.9 0.0 copy-done.2
  49.9 0.9 maximum_convert_fusion
  50.8 15.7 %all_gather.9 = bf16[384,1024]{1,0:T(8,128)(2,1)S(1)} all-gather(bf16[48,1024]{1,0:T(8,128)(2,1)S(1)} %maximum_convert_fusion), channel_id=1, replica_groups=mesh['width'=8,'lat'=4] {'width'}, dimensions={0}, use_global_device_ids=true | all-gather | bytes 884736 | tf_op jit(solution)/shard_map/all_gather | solution.py:27
  66.5 0.0 copy-start.1
  66.5 0.0 copy-start.3
  66.5 5.8 %fusion.7 = f32[384,2048]{1,0:T(8,128)} fusion(bf16[384,1024]{1,0:T(8,128)(2,1)S(1)} %all_gather.9, bf16[1024,2048]{1,0:T(8,128)(2,1)} %param.8), kind=kOutput, calls=%fused_computation.18 | convolution fusion | flops 1610612736 | bytes 8126464 | tf_op jit(solution)/shard_map/dot_general | solution.py:30
  72.3 0.0 reduce-scatter.6.cloned.1.call-update
  72.3 0.0 all-gather.2.cloned.1.call-start
  72.3 42.5 %reduce-scatter.6.cloned.1.call-done = f32[96,2048]{1,0:T(8,128)} async-done(((f32[384,2048]{1,0:T(8,128)}), f32[96,2048]{1,0:T(8,128)}) %reduce-scatter.6.cloned.1.call-update) | async-done | bytes 786448 | tf_op jit(solution)/shard_map/reduce_scatter | solution.py:29
  114.8 0.0 copy-done.1
  114.8 0.0 copy-done.3
  114.8 2.0 subtract_convert_fusion
  116.8 0.0 all-gather.2.cloned.1.call-update
  116.9 0.0 reduce-scatter.8.cloned.1.call-start
  116.9 31.2 %all-gather.2.cloned.1.call-done = bf16[384,2048]{1,0:T(8,128)(2,1)} async-done(((bf16[96,2048]{1,0:T(8,128)(2,1)}), bf16[384,2048]{1,0:T(8,128)(2,1)}) %all-gather.2.cloned.1.call-update) | async-done | bytes 1572880 | tf_op jit(solution)/shard_map/all_gather | solution.py:38
  148.1 5.6 %fusion.8 = f32[384,1024]{1,0:T(8,128)} fusion(bf16[384,2048]{1,0:T(8,128)(2,1)} %all-gather.2.cloned.1.call-done, bf16[1024,2048]{1,0:T(8,128)(2,1)} %param.8), kind=kOutput, calls=%fused_computation.19 | convolution fusion | flops 1610612736 | bytes 7340032 | tf_op jit(solution)/shard_map/dot_general | solution.py:42
  153.7 0.0 reduce-scatter.8.cloned.1.call-update
  153.8 7.8 %fusion = (f32[1024]{0:T(1024)S(1)}, f32[1024]{0:T(1024)S(1)}, f32[1024]{0:T(1024)S(1)}, f32[1024,2048]{1,0:T(8,128)}) fusion(bf16[1024,2048]{1,0:T(8,128)(2,1)} %param.8, bf16[384,1024]{1,0:T(8,128)(2,1)S(1)} %all_gather.9, bf16[384,2048]{1,0:T(8,128)(2,1)} %all-gather.2.cloned.1.call-done), kind=kOutput, calls=%fused_computation.4 | convolution fusion | flops 1625289728 | bytes 14954496 | tf_op jit(solution)/shard_map/dot_general | solution.py:56
  161.6 28.5 %all-reduce = (f32[1024]{0:T(1024)S(1)}, f32[1024]{0:T(1024)S(1)}, f32[1024]{0:T(1024)S(1)}) all-reduce(f32[1024]{0:T(1024)S(1)} %get-tuple-element.6, f32[1024]{0:T(1024)S(1)} %get-tuple-element.5, f32[1024]{0:T(1024)S(1)} %get-tuple-element.4), channel_id=1, replica_groups=mesh['width'=8,'lat'=4] {'width'}, use_global_device_ids=true, to_apply=%region_6.7 | all-reduce | flops 3072 | bytes 24576 | tf_op jit(solution)/shard_map/psum | solution.py:60
  190.1 0.0 copy-start
  190.1 7.2 %fusion.5 = bf16[1024,2048]{1,0:T(8,128)(2,1)} fusion(f32[1024,2048]{1,0:T(8,128)} %get-tuple-element.12, bf16[1024,2048]{1,0:T(8,128)(2,1)} %param.8, f32[1024]{0:T(1024)S(1)} %get-tuple-element.11, f32[1024]{0:T(1024)S(1)} %get-tuple-element.10), kind=kLoop, calls=%fused_computation.10 | loop fusion | flops 14680064 | bytes 16785408 | tf_op jit(solution)/shard_map/convert_element_type | solution.py:76
  197.3 0.0 reduce-scatter.8.cloned.1.call-done
  197.3 0.0 copy-done
  197.3 1.0 select_convert_fusion
  198.3 15.7 %all_gather.11 = bf16[384,1024]{1,0:T(8,128)(2,1)S(1)} all-gather(bf16[48,1024]{1,0:T(8,128)(2,1)S(1)} %select_convert_fusion), channel_id=1, replica_groups=mesh['width'=8,'lat'=4] {'width'}, dimensions={0}, use_global_device_ids=true | all-gather | bytes 884736 | tf_op jit(solution)/shard_map/all_gather | solution.py:52
  214.0 4.3 %convert_bitcast_fusion = bf16[2048,1024]{0,1:T(8,128)(2,1)} fusion(bf16[384,1024]{1,0:T(8,128)(2,1)S(1)} %all_gather.11, bf16[384,2048]{1,0:T(8,128)(2,1)S(1)} %copy-done.1), kind=kOutput, calls=%fused_computation.11 | convolution fusion | flops 1612709888 | bytes 6553600 | tf_op jit(solution)/shard_map/dot_general | solution.py:53
  218.3 6.4 %copy.7 = bf16[2048,1024]{1,0:T(8,128)(2,1)} copy(bf16[2048,1024]{0,1:T(8,128)(2,1)} %convert_bitcast_fusion) | data formatting | bytes 8388608
  (1 shorter events, 0.0 us)
Async XLA Ops:
  7.2 42.7 %copy-start.2 = (f32[1024]{0:T(1024)S(1)}, f32[1024]{0:T(1024)}, u32[]{:S(2)}) copy-start(f32[1024]{0:T(1024)} %param.7) | copy-start | bytes 12292
  7.2 42.7 %reduce-scatter.4.cloned.1.call-start = ((), (), s32[]{:S(2)}) async-start(), calls=%async_computation.3 | async-start | bytes 1769472 | tf_op jit(solution)/shard_map/reduce_scatter | solution.py:17
  12.8 102.0 %reduce-scatter.6.cloned.1.call-start = ((), (), s32[]{:S(2)}) async-start(), calls=%async_computation.4 | async-start | bytes 3932160 | tf_op jit(solution)/shard_map/reduce_scatter | solution.py:29
  66.5 48.3 %copy-start.1 = (bf16[384,2048]{1,0:T(8,128)(2,1)S(1)}, bf16[384,2048]{1,0:T(8,128)(2,1)}, u32[]{:S(2)}) copy-start(bf16[384,2048]{1,0:T(8,128)(2,1)} %param.5) | copy-start | bytes 4718596
  66.5 48.3 %copy-start.3 = (f32[2048]{0:T(1024)S(1)}, f32[2048]{0:T(1024)}, u32[]{:S(2)}) copy-start(f32[2048]{0:T(1024)} %param.9) | copy-start | bytes 24580
  72.3 75.8 %all-gather.2.cloned.1.call-start = ((), (), s32[]{:S(2)}) async-start(), calls=%async_computation.5 | async-start | bytes 1966080 | tf_op jit(solution)/shard_map/all_gather | solution.py:38
  116.9 80.4 %reduce-scatter.8.cloned.1.call-start = ((), (), s32[]{:S(2)}) async-start(), calls=%async_computation.6 | async-start | bytes 1769472 | tf_op jit(solution)/shard_map/reduce_scatter | solution.py:41
  190.1 7.2 %copy-start = (f32[48,1024]{1,0:T(8,128)S(1)}, f32[48,1024]{1,0:T(8,128)}, u32[]{:S(2)}) copy-start(f32[48,1024]{1,0:T(8,128)} %reduce-scatter.4.cloned.1.call-done) | copy-start | bytes 589828
Sparse Core Ops, SparseCore 0:
  13.0 36.8 reduce-scatter.3
  72.4 42.3 reduce-scatter.5
  117.3 30.8 all-gather.1
  153.9 34.4 reduce-scatter.7
where the time goes:
time: 232 us; the launch traced here: 231 us
  waiting for transfers between devices  111 us (48%)
  blocking collectives  59.9 us (26%)
  matrix products  29.1 us (13%)
  between operations  13.8 us (6%)
  other arithmetic  11.1 us (5%)
  local copies, waits for them, and re-layouts  6.41 us (3%)
    reduce_scatter x1, waiting for transfers between devices, per_device(): lax.psum_scatter(jnp.dot(rows, decoder, preferred_element_type=jnp.float3...  42.5 us
    reduce_scatter x1, waiting for transfers between devices, per_device(): lax.psum_scatter(jnp.dot(rows, encoder, preferred_element_type=jnp.float3...  37 us
    all_gather x1, waiting for transfers between devices, per_device(): error = lax.all_gather(error_part, 'lat', axis=0, tiled=True)  31.2 us
    psum x1, blocking collectives, per_device(): lax.psum((jnp.sum(weight * weight, axis=1), jnp.sum(grad * weight, axis=1...  28.5 us
    all_gather x1, blocking collectives, per_device(): dpre = lax.all_gather(dpre_part, 'width', axis=0, tiled=True)  15.7 us
    all_gather x1, blocking collectives, per_device(): acts = lax.all_gather(act_rows, 'width', axis=0, tiled=True)  15.7 us
    dot_general x1, matrix products, per_device(): lax.dot_general(acts, error, (((0,), (0,)), ((), ())), preferred_element_...  7.82 us
    convert_element_type x1, other arithmetic, per_device(): (moved / jnp.sqrt(squared + EPS)[:, None]).astype(jnp.bfloat16)  7.18 us
  transfers between devices with their start and end apart: 4, of which 3 were waited for; matrix products, arithmetic and copies ran while one was open for 6% of the time, Pallas kernels for 0%

commit v1 on v0

--- a/solution.py
+++ b/solution.py
@@ -1,14 +1,451 @@
+import functools
+
 import jax
 import jax.numpy as jnp
 from jax import lax
+from jax.experimental import pallas as pl
+from jax.experimental.pallas import tpu as pltpu
 from jax.sharding import PartitionSpec as P
 
 EPS = 1e-06
 STEP = 0.0003
 PENALTY = 0.5
-
-
-def per_device(residuals, encoder, enc_bias, decoder, dec_bias):
+MESH = pl.DeviceIdType.MESH
+F32, BF16 = jnp.float32, jnp.bfloat16
+NT = (((1,), (1,)), ((), ()))
+
+
+def step_kernel(
+    Z, NL, NK, NN,
+    res_h, enc_h, bias, dec_h, dbias,
+    nd_o, dp_o, rt_o,
+    res_v, enc_v, dec_v, stA, rxA, sA, rA, preS, acts, actsT, rt_v,
+    rf, sB, rB, err, dacc, sD, rxD, sS, rD, dp, grad, sacc, stv, rst, ss, rs2, nd_v,
+    in_sem, out_sem,
+    a1s, a1r, a2s, a2r, a3s, a3r, a4s, a4r,
+    bs, br, cs, cr,
+    d1s, d1r, d2s, d2r, d3s, d3r, d4s, d4r,
+    e1s, e1r, e2s, e2r,
+):
+    T, DW = res_v.shape
+    KB = acts.shape[-1]
+    TB = acts.shape[-2]
+    TL = err.shape[2]
+    NB = err.shape[3]
+    w = lax.axis_index("width")
+    l = lax.axis_index("lat")
+    z, c = w // 2, w % 2
+    pc = 1 - c
+    partner = (z * 2 + pc, l)
+
+    def zdev(o):
+        return ((z + o) % Z) * 2 + c, l
+
+    def lat_to(o):
+        return ((l // 2 + o // 2) % (NL // 2)) * 2 + (l % 2 + o % 2) % 2
+
+    def lat_from(o):
+        return ((l // 2 + NL // 2 - o // 2) % (NL // 2)) * 2 + (l % 2 + o % 2) % 2
+
+    def rc(src, dst, ssem, rsem, dev):
+        return pltpu.make_async_remote_copy(
+            src_ref=src, dst_ref=dst, send_sem=ssem, recv_sem=rsem,
+            device_id=dev, device_id_type=MESH,
+        )
+
+    def loop(n, f):
+        lax.fori_loop(0, n, lambda i, _: (f(i), 0)[1], 0)
+
+    c_res = pltpu.make_async_copy(res_h, res_v, in_sem.at[0])
+    c_res.start()
+
+    def enc_copy(k):
+        return pltpu.make_async_copy(
+            enc_h.at[:, pl.ds(pl.multiple_of(k * KB, KB), KB)], enc_v.at[k], in_sem.at[1 + k]
+        )
+
+    def dec_copy(n):
+        return pltpu.make_async_copy(
+            dec_h.at[:, pl.ds(pl.multiple_of(n * NB, NB), NB)], dec_v.at[n], in_sem.at[1 + NK + n]
+        )
+
+    for k in range(NK):
+        enc_copy(k).start()
+    for n in range(NN):
+        dec_copy(n).start()
+
+    barrier = pltpu.get_barrier_semaphore()
+    pl.semaphore_signal(barrier, inc=1, device_id=partner, device_id_type=MESH)
+    for o in range(1, Z):
+        pl.semaphore_signal(barrier, inc=1, device_id=zdev(o), device_id_type=MESH)
+    for o in range(1, NL):
+        pl.semaphore_signal(barrier, inc=1, device_id=(w, lat_to(o)), device_id_type=MESH)
+
+    def a1(k):
+        return rc(stA.at[k, pc], rxA.at[k], a1s.at[k], a1r.at[k], partner)
+
+    def a2(k, o):
+        return rc(sA.at[k, (z + o) % Z], rA.at[k, o], a2s.at[k, o], a2r.at[k, o], zdev(o))
+
+    def a3(k, o):
+        return rc(acts.at[k, c, z], acts.at[k, c, z], a3s.at[k, o], a3r.at[k, o], zdev(o))
+
+    def a3in(k, o):
+        dst = acts.at[k, c, (z + Z - o) % Z]
+        return rc(dst, dst, a3s.at[k, o], a3r.at[k, o], zdev(o))
+
+    def a4(k):
+        return rc(acts.at[k, c], acts.at[k, c], a4s.at[k], a4r.at[k], partner)
+
+    def a4in(k):
+        return rc(acts.at[k, pc], acts.at[k, pc], a4s.at[k], a4r.at[k], partner)
+
+    def combine_a(k):
+        a1(k).wait_recv()
+        sA[k] = stA[k, c] + rxA[k]
+        for o in range(1, Z):
+            a2(k, o).start()
+
+    c_res.wait()
+    pl.semaphore_wait(barrier, 1 + (Z - 1) + (NL - 1))
+
+    def pre_step(k):
+        enc_copy(k).wait()
+        p = jnp.dot(res_v[...], enc_v[k], preferred_element_type=F32)
+        stA[k] = p.reshape(2, Z, TB, KB)
+        a1(k).start()
+
+        @pl.when(k > 0)
+        def _():
+            combine_a(k - 1)
+
+    loop(NK, pre_step)
+    combine_a(NK - 1)
+
+    def fwd_a(k):
+        for o in range(1, Z):
+            a3in(k, o).wait_recv()
+        a4(k).start()
+
+    def act_step(k):
+        for o in range(1, Z):
+            a2(k, o).wait_recv()
+        pre = sA[k, z]
+        for o in range(1, Z):
+            pre = pre + rA[k, o]
+        pre = pre + bias[k]
+        preS[k] = pre
+        acts[k, c, z] = jnp.maximum(pre, 0.0).astype(BF16)
+        for o in range(1, Z):
+            a3(k, o).start()
+
+        @pl.when(k > 0)
+        def _():
+            fwd_a(k - 1)
+
+    RB = NB
+
+    def rt_step(n):
+        rt_v[n] = res_v[:, pl.ds(pl.multiple_of(n * RB, RB), RB)].T
+
+    loop(NN, rt_step)
+    rt_copy = pltpu.make_async_copy(rt_v, rt_o, out_sem.at[0])
+    rt_copy.start()
+
+    loop(NK, act_step)
+    fwd_a(NK - 1)
+    for n in range(NN):
+        dec_copy(n).wait()
+    loop(NK, lambda k: a4in(k).wait_recv())
+
+    def b1(n, o):
+        return rc(sB.at[n, lat_to(o)], rB.at[n, o], bs.at[n, o], br.at[n, o], (w, lat_to(o)))
+
+    def c1(n, o):
+        return rc(err.at[n, l], err.at[n, l], cs.at[n, o], cr.at[n, o], (w, lat_to(o)))
+
+    def c1in(n, o):
+        dst = err.at[n, lat_from(o)]
+        return rc(dst, dst, cs.at[n, o], cr.at[n, o], (w, lat_to(o)))
+
+    def rec_step(n):
+        a = jnp.concatenate([acts[k].reshape(T, KB) for k in range(NK)], axis=1)
+        r = jnp.dot(a, dec_v[n], preferred_element_type=F32).reshape(NL, TL, NB)
+        rf[n] = r
+        sB[n] = r.astype(BF16)
+        for o in range(1, NL):
+            b1(n, o).start()
+
+    loop(NN, rec_step)
+
+    def at_step(k):
+        actsT[k] = acts[k].reshape(T, KB).T
+        dacc[k] = jnp.zeros(dacc.shape[1:], F32)
+        for s in range(3):
+            sacc[s, k] = jnp.zeros(sacc.shape[2:], F32)
+
+    loop(NK, at_step)
+
+    def err_step(n):
+        for o in range(1, NL):
+            b1(n, o).wait_recv()
+        r = rf[n, l]
+        for o in range(1, NL):
+            r = r + rB[n, o].astype(F32)
+        own = res_v[
+            pl.ds(pl.multiple_of(l * TL, TL), TL), pl.ds(pl.multiple_of(n * NB, NB), NB)
+        ]
+        err[n, l] = (r + dbias[n] - own.astype(F32)).astype(BF16)
+        for o in range(1, NL):
+            c1(n, o).start()
+
+    loop(NN, err_step)
+
+    def dacts_part(n, k):
+        e = err[n].reshape(T, NB)
+        d = lax.dot_general(
+            e, dec_v[n, pl.ds(pl.multiple_of(k * KB, KB), KB), :], NT, preferred_element_type=F32
+        )
+        return dacc[k] + d.reshape(2, Z, TB, KB)
+
+    def grad_part(n, k):
+        g = jnp.dot(actsT[k], err[n].reshape(T, NB), preferred_element_type=F32)
+        grad[n, k] = g
+        wt = dec_v[n, pl.ds(pl.multiple_of(k * KB, KB), KB), :].astype(F32)
+        for s, prod in enumerate((wt * wt, g * wt, g * g)):
+            part = prod[:, 0:128]
+            for j in range(1, NB // 128):
+                part = part + prod[:, j * 128:(j + 1) * 128]
+            sacc[s, k] += part
+
+    def err_wait(n):
+        for o in range(1, NL):
+            c1in(n, o).wait_recv()
+
+    def n_step(n):
+        err_wait(n)
+
+        def k_step(k):
+            dacc[k] = dacts_part(n, k)
+            grad_part(n, k)
+
+        loop(NK, k_step)
+
+    loop(NN - 1, n_step)
+
+    def d1(k):
+        return rc(sD.at[k, pc], rxD.at[k], d1s.at[k], d1r.at[k], partner)
+
+    def d2(k, o):
+        return rc(sS.at[k, (z + o) % Z], rD.at[k, o], d2s.at[k, o], d2r.at[k, o], zdev(o))
+
+    def d3(k, o):
+        return rc(dp.at[k, c, z], dp.at[k, c, z], d3s.at[k, o], d3r.at[k, o], zdev(o))
+
+    def d3in(k, o):
+        dst = dp.at[k, c, (z + Z - o) % Z]
+        return rc(dst, dst, d3s.at[k, o], d3r.at[k, o], zdev(o))
+
+    def d4(k):
+        return rc(dp.at[k, c], dp.at[k, c], d4s.at[k], d4r.at[k], partner)
+
+    def d4in(k):
+        return rc(dp.at[k, pc], dp.at[k, pc], d4s.at[k], d4r.at[k], partner)
+
+    def combine_d(k):
+        d1(k).wait_recv()
+        s = dacc[k, c] + rxD[k].astype(F32)
+        dacc[k, c] = s
+        sS[k] = s.astype(BF16)
+        for o in range(1, Z):
+            d2(k, o).start()
+
+    last = NN - 1
+    err_wait(last)
+
+    def d_step(k):
+        v = dacts_part(last, k)
+        dacc[k] = v
+        sD[k] = v.astype(BF16)
+        d1(k).start()
+
+        @pl.when(k > 0)
+        def _():
+            combine_d(k - 1)
+
+    loop(NK, d_step)
+    combine_d(NK - 1)
+
+    def g_step(k):
+        grad_part(last, k)
+        for s in range(3):
+            stv[k, s:s + 1, :] = jnp.sum(sacc[s, k].T, axis=0, keepdims=True)
+        stv[k, 3:8, :] = jnp.zeros((5, KB), F32)
+
+    def dp_step(k):
+        for o in range(1, Z):
+            d2(k, o).wait_recv()
+        v = dacc[k, c, z]
+        for o in range(1, Z):
+            v = v + rD[k, o].astype(F32)
+        dp[k, c, z] = jnp.where(preS[k] > 0.0, v + PENALTY, 0.0).astype(BF16)
+        for o in range(1, Z):
+            d3(k, o).start()
+
+    def gd_step(k):
+        g_step(k)
+        dp_step(k)
+
+    loop(NK, gd_step)
+
+    e1 = rc(stv, rst, e1s, e1r, partner)
+    e1.start()
+
+    def e2(o):
+        return rc(ss, rs2.at[o], e2s.at[o], e2r.at[o], zdev(o))
+
+    e1.wait_recv()
+    ss[...] = stv[...] + rst[...]
+    for o in range(1, Z):
+        e2(o).start()
+
+    def fwd_d(k):
+        for o in range(1, Z):
+            d3in(k, o).wait_recv()
+        d4(k).start()
+
+    loop(NK, fwd_d)
+    for o in range(1, Z):
+        e2(o).wait_recv()
+
+    def nd_copy(k):
+        return pltpu.make_async_copy(
+            nd_v.at[k], nd_o.at[pl.ds(pl.multiple_of(k * KB, KB), KB), :], out_sem.at[2 + k]
+        )
+
+    def nd_step(k):
+        t = ss[k]
+        for o in range(1, Z):
+            t = t + rs2[o, k]
+        ww, gw, gg = t[0:1], t[1:2], t[2:3]
+        coef = gw / (ww + EPS)
+        sq = (
+            ww
+            - 2.0 * STEP * (gw - coef * ww)
+            + STEP * STEP * (gg - 2.0 * coef * gw + coef * coef * ww)
+        )
+        inv = 1.0 / jnp.sqrt(sq + EPS)
+        up = jnp.broadcast_to((1.0 + STEP * coef) * inv, (128, KB)).T
+        down = jnp.broadcast_to(STEP * inv, (128, KB)).T
+        for n in range(NN):
+            for j in range(NB // 128):
+                wt = dec_v[n, pl.ds(pl.multiple_of(k * KB, KB), KB), j * 128:(j + 1) * 128]
+                g = grad[n, k, :, j * 128:(j + 1) * 128]
+                first = n * NB + j * 128
+                nd_v[k, :, first:first + 128] = (wt.astype(F32) * up - g * down).astype(BF16)
+        nd_copy(k).start()
+
+    loop(NK, nd_step)
+    loop(NK, lambda k: d4in(k).wait_recv())
+    dp_copy = pltpu.make_async_copy(dp, dp_o, out_sem.at[1])
+    dp_copy.start()
+
+    def drain(k):
+        for first in (a1, a4, d1, d4):
+            first(k).wait_send()
+        for o in range(1, Z):
+            for each in (a2, a3, d2, d3):
+                each(k, o).wait_send()
+        nd_copy(k).wait()
+
+    def drain_n(n):
+        for o in range(1, NL):
+            b1(n, o).wait_send()
+            c1(n, o).wait_send()
+
+    loop(NK, drain)
+    loop(NN, drain_n)
+    e1.wait_send()
+    for o in range(1, Z):
+        e2(o).wait_send()
+    rt_copy.wait()
+    dp_copy.wait()
+
+
+def enc_grad_kernel(rt, dp, out):
+    for k in range(dp.shape[0]):
+        kb = dp.shape[2]
+        out[:, k * kb:(k + 1) * kb] = jnp.dot(
+            rt[0], dp[k], preferred_element_type=F32
+        ).astype(BF16)
+
+
+def fused(W, NL, residuals, encoder, enc_bias, decoder, dec_bias):
+    T, DW = residuals.shape
+    LL = encoder.shape[1]
+    Z = W // 2
+    NK, NN = 4, 4
+    KB, NB = LL // NK, DW // NN
+    TB, TL = T // W, T // NL
+    V = pltpu.VMEM
+    dma = pltpu.SemaphoreType.DMA
+    scratch = [
+        V((T, DW), BF16), V((NK, DW, KB), BF16), V((NN, LL, NB), BF16),
+        V((NK, 2, Z, TB, KB), F32), V((NK, Z, TB, KB), F32), V((NK, Z, TB, KB), F32),
+        V((NK, Z, TB, KB), F32), V((NK, TB, KB), F32),
+        V((NK, 2, Z, TB, KB), BF16), V((NK, KB, T), BF16), V((NN, NB, T), BF16),
+        V((NN, NL, TL, NB), F32), V((NN, NL, TL, NB), BF16), V((NN, NL, TL, NB), BF16),
+        V((NN, NL, TL, NB), BF16),
+        V((NK, 2, Z, TB, KB), F32), V((NK, 2, Z, TB, KB), BF16), V((NK, Z, TB, KB), BF16),
+        V((NK, Z, TB, KB), BF16), V((NK, Z, TB, KB), BF16), V((NK, 2, Z, TB, KB), BF16),
+        V((NN, NK, KB, NB), F32), V((3, NK, KB, 128), F32),
+        V((NK, 8, KB), F32), V((NK, 8, KB), F32), V((NK, 8, KB), F32), V((Z, NK, 8, KB), F32),
+        V((NK, KB, DW), BF16),
+        dma((1 + NK + NN,)), dma((2 + NK,)),
+        dma((NK,)), dma((NK,)), dma((NK, Z)), dma((NK, Z)), dma((NK, Z)), dma((NK, Z)),
+        dma((NK,)), dma((NK,)),
+        dma((NN, NL)), dma((NN, NL)), dma((NN, NL)), dma((NN, NL)),
+        dma((NK,)), dma((NK,)), dma((NK, Z)), dma((NK, Z)), dma((NK, Z)), dma((NK, Z)),
+        dma((NK,)), dma((NK,)),
+        dma, dma, dma((Z,)), dma((Z,)),
+    ]
+    hbm = pl.BlockSpec(memory_space=pl.ANY)
+    vm = pl.BlockSpec(memory_space=pltpu.VMEM)
+    new_decoder, dp, rt = pl.pallas_call(
+        functools.partial(step_kernel, Z, NL, NK, NN),
+        out_shape=(
+            jax.ShapeDtypeStruct((LL, DW), BF16),
+            jax.ShapeDtypeStruct((NK, 2, Z, TB, KB), BF16),
+            jax.ShapeDtypeStruct((NN, NB, T), BF16),
+        ),
+        in_specs=[hbm, hbm, vm, hbm, vm],
+        out_specs=(hbm, hbm, hbm),
+        scratch_shapes=scratch,
+        compiler_params=pltpu.CompilerParams(
+            collective_id=0, has_side_effects=True, vmem_limit_bytes=60 * 2**20
+        ),
+        name="sae_step",
+    )(residuals, encoder, enc_bias.reshape(NK, 1, KB), decoder, dec_bias.reshape(NN, 1, NB))
+    enc_grad = pl.pallas_call(
+        enc_grad_kernel,
+        grid=(NN,),
+        out_shape=jax.ShapeDtypeStruct((DW, LL), BF16),
+        in_specs=[
+            pl.BlockSpec((1, NB, T), lambda i: (i, 0, 0)),
+            pl.BlockSpec((NK, T, KB), lambda i: (0, 0, 0)),
+        ],
+        out_specs=pl.BlockSpec((NB, LL), lambda i: (i, 0)),
+        compiler_params=pltpu.CompilerParams(vmem_limit_bytes=24 * 2**20),
+        cost_estimate=pl.CostEstimate(
+            flops=2 * T * DW * LL, bytes_accessed=2 * (T * DW + T * LL + DW * LL),
+            transcendentals=0,
+        ),
+        name="enc_grad",
+    )(rt, dp.reshape(NK, T, KB))
+    return enc_grad, new_decoder
+
+
+def plain(residuals, encoder, enc_bias, decoder, dec_bias):
     tokens = residuals.shape[0]
     lat_count = lax.axis_size("lat")
     lat_rows = tokens // lat_count
@@ -77,9 +514,19 @@
     return (enc_grad, new_decoder)
 
 
+def per_device(W, NL, residuals, encoder, enc_bias, decoder, dec_bias):
+    T, DW = residuals.shape
+    LL = encoder.shape[1]
+    args = (residuals, encoder, enc_bias, decoder, dec_bias)
+    fits = W % 2 == 0 and NL % 2 == 0 and T % (16 * W) == 0 and T % (16 * NL) == 0
+    if fits and DW % 512 == 0 and LL % 512 == 0 and T % 128 == 0:
+        return fused(W, NL, *args)
+    return plain(*args)
+
+
 def solution(mesh):
     return jax.shard_map(
-        per_device,
+        functools.partial(per_device, mesh.shape["width"], mesh.shape["lat"]),
         mesh=mesh,
         in_specs=(P(None, "width"), P("width", "lat"), P("lat"), P("lat", "width"), P("width")),
         out_specs=(P("width", "lat"), P("lat", "width")),

time: 232 us -> 111 us (0.48)
  waiting for transfers between devices: 111 us -> 0 us
  Pallas kernels: 0 us -> 106 us
  blocking collectives: 59.9 us -> 0 us
  matrix products: 29.1 us -> 0 us
  between operations: 13.8 us -> 0.65 us
  other arithmetic: 11.1 us -> 0 us
    pallas_call x0 -> x2, Pallas kernels: none -> 106 us  [the longest x1 102 us: fused(): pl.pallas_call(functools.partial(step_kernel, Z, NL, NK, NN), out_shape=(...]
    reduce_scatter x3 -> x0, waiting for transfers between devices: 79.5 us -> none  [the longest x1 42.5 us: per_device(): lax.psum_scatter(jnp.dot(rows, decoder, preferred_element_type=jnp.float3...]
    all_gather x2 -> x0, blocking collectives: 31.4 us -> none  [the longest x1 15.7 us: per_device(): dpre = lax.all_gather(dpre_part, 'width', axis=0, tiled=True)]
    all_gather x1 -> x0, waiting for transfers between devices: 31.2 us -> none  [per_device(): error = lax.all_gather(error_part, 'lat', axis=0, tiled=True)]
    dot_general x5 -> x0, matrix products: 29.1 us -> none  [the longest x1 7.82 us: per_device(): lax.dot_general(acts, error, (((0,), (0,)), ((), ())), preferred_element_...]
    psum x1 -> x0, blocking collectives: 28.5 us -> none  [per_device(): lax.psum((jnp.sum(weight * weight, axis=1), jnp.sum(grad * weight, axis=1...]
    convert_element_type x4 -> x0, other arithmetic: 11.1 us -> none  [the longest x1 7.18 us: per_device(): (moved / jnp.sqrt(squared + EPS)[:, None]).astype(jnp.bfloat16)]
    unnamed x9 -> x7, local copies, waits for them, and re-layouts: 6.41 us -> 4.55 us
  transfers between devices with their start and end apart: 4 -> 0, of which waited for: 3 -> 0; matrix products, arithmetic and copies ran while one was open for 6% -> 0% of each run, Pallas kernels for 0% -> 0%
where the time goes in v1:
time: 111 us
  Pallas kernels  106 us (95%)
  local copies, waits for them, and re-layouts  4.55 us (4%)
    pallas_call x1, Pallas kernels, fused(): pl.pallas_call(functools.partial(step_kernel, Z, NL, NK, NN), out_shape=(...  102 us
    unnamed x7, local copies, waits for them, and re-layouts  4.55 us
    pallas_call x1, Pallas kernels, fused(): pl.pallas_call(enc_grad_kernel, grid=(NN,), out_shape=jax.ShapeDtypeStruc...  4.08 us

profile of v1, /device:TPU:0, one launch (start us, length us, event | category | flops | bytes accessed | tf_op | source)
XLA Modules:
  0.0 110.8 jit_solution(14290239518861652924)
XLA Ops:
  0.6 101.5 %sae_step.1 = (bf16[1024,2048]{1,0:T(8,128)(2,1)}, bf16[4,2,4,48,256]{4,3,2,1,0:T(8,128)(2,1)}, bf16[4,512,384]{2,1,0:T(8,128)(2,1)}) custom-call(bf16[384,2048]{1,0:T(8,128)(2,1)} %res_h.1, bf16[2048,1024]{1,0:T(8,128)(2,1)} %enc_h.1, f32[4,1,256]{2,1,0:T(1,128)} %bitcast.5, bf16[1024,2048]{1,0:T(8,128)(2,1)} %dec_h.1, f32[4,1,512]{2,1,0:T(1,128)} %bitcast.4), custom_call_target="tpu_custom_call" | custom-call | tf_op jit(solution)/shard_map/sae_step/pallas_call | solution.py:414
  102.1 0.0 copy-start
  102.2 1.4 %copy-done = bf16[4,512,384]{2,1,0:T(8,128)(2,1)S(1)} copy-done((bf16[4,512,384]{2,1,0:T(8,128)(2,1)S(1)}, bf16[4,512,384]{2,1,0:T(8,128)(2,1)}, u32[]{:S(2)}) %copy-start) | copy-done | bytes 1572888
  103.5 0.0 copy-start.1
  103.6 1.1 %copy-done.1 = bf16[4,2,4,48,256]{4,3,2,1,0:T(8,128)(2,1)S(1)} copy-done((bf16[4,2,4,48,256]{4,3,2,1,0:T(8,128)(2,1)S(1)}, bf16[4,2,4,48,256]{4,3,2,1,0:T(8,128)(2,1)}, u32[]{:S(2)}) %copy-start.1) | copy-done | bytes 786456
  104.7 0.0 copy-start.2
  104.7 4.1 %enc_grad.1 = bf16[2048,1024]{1,0:T(8,128)(2,1)} custom-call(bf16[4,512,384]{2,1,0:T(8,128)(2,1)S(1)} %copy-done, bf16[4,384,256]{2,1,0:T(8,128)(2,1)S(1)} %bitcast.3), custom_call_target="tpu_custom_call" | custom-call | flops 1610612736 | bytes 6553600 | tf_op jit(solution)/shard_map/enc_grad/pallas_call | solution.py:429
  108.8 0.0 copy-done.2
  108.8 2.0 %copy.8 = bf16[1024,2048]{1,0:T(8,128)(2,1)} copy(bf16[1024,2048]{1,0:T(8,128)(2,1)S(1)} %copy-done.2) | data formatting | bytes 8388608
Async XLA Ops:
  102.1 1.4 %copy-start = (bf16[4,512,384]{2,1,0:T(8,128)(2,1)S(1)}, bf16[4,512,384]{2,1,0:T(8,128)(2,1)}, u32[]{:S(2)}) copy-start(bf16[4,512,384]{2,1,0:T(8,128)(2,1)} %get-tuple-element.5.rt) | copy-start | bytes 4718596
  103.5 1.1 %copy-start.1 = (bf16[4,2,4,48,256]{4,3,2,1,0:T(8,128)(2,1)S(1)}, bf16[4,2,4,48,256]{4,3,2,1,0:T(8,128)(2,1)}, u32[]{:S(2)}) copy-start(bf16[4,2,4,48,256]{4,3,2,1,0:T(8,128)(2,1)} %get-tuple-element.6) | copy-start | bytes 2359300
  104.7 4.1 %copy-start.2 = (bf16[1024,2048]{1,0:T(8,128)(2,1)S(1)}, bf16[1024,2048]{1,0:T(8,128)(2,1)}, u32[]{:S(2)}) copy-start(bf16[1024,2048]{1,0:T(8,128)(2,1)} %get-tuple-element.11) | copy-start | bytes 12582916

commit v2 on v1

v2 whole, which is shorter than its diff:
```python
import functools

import jax
import jax.numpy as jnp
from jax import lax
from jax.experimental import pallas as pl
from jax.experimental.pallas import tpu as pltpu
from jax.sharding import PartitionSpec as P

EPS = 1e-06
STEP = 0.0003
PENALTY = 0.5
MESH = pl.DeviceIdType.MESH
F32, BF16 = jnp.float32, jnp.bfloat16
NT = (((1,), (1,)), ((), ()))


def step_kernel(
    Z, NL, NK, NN,
    res_h, enc_h, bias, dec_h, dbias,
    nd_o, dp_o, rt_o,
    res_v, enc_v, dec_v, stA, rxA, sA, rA, preS, acts, actsT, rt_v,
    rf, sB, rB, err, dacc, sD, rxD, sS, rD, dp, grad, sacc, stv, rst, ss, rs2, nd_v,
    in_sem, out_sem,
    a1s, a1r, a2s, a2r, a3s, a3r, a4s, a4r,
    bs, br, cs, cr,
    d1s, d1r, d2s, d2r, d3s, d3r, d4s, d4r,
    e1s, e1r, e2s, e2r,
):
    T, DW = res_v.shape
    H = acts.shape[0]
    TH = T // H
    TB, KC = acts.shape[-2:]
    KB = 2 * KC
    TL, NB = err.shape[-2:]
    w = lax.axis_index("width")
    l = lax.axis_index("lat")
    z, c = w // 2, w % 2
    pc = 1 - c
    partner = (z * 2 + pc, l)

    def zdev(o):
        return ((z + o) % Z) * 2 + c, l

    def lat_to(o):
        return ((l // 2 + o // 2) % (NL // 2)) * 2 + (l % 2 + o % 2) % 2

    def lat_from(o):
        return ((l // 2 + NL // 2 - o // 2) % (NL // 2)) * 2 + (l % 2 + o % 2) % 2

    def rc(src, dst, ssem, rsem, dev):
        return pltpu.make_async_remote_copy(
            src_ref=src, dst_ref=dst, send_sem=ssem, recv_sem=rsem,
            device_id=dev, device_id_type=MESH,
        )

    def loop(n, f):
        lax.fori_loop(0, n, lambda i, _: (f(i), 0)[1], 0)

    c_res = pltpu.make_async_copy(res_h, res_v, in_sem.at[0])
    c_res.start()

    def enc_copy(k):
        return pltpu.make_async_copy(
            enc_h.at[:, pl.ds(pl.multiple_of(k * KB, KB), KB)], enc_v.at[k], in_sem.at[1 + k]
        )

    def dec_copy(n):
        return pltpu.make_async_copy(
            dec_h.at[:, pl.ds(pl.multiple_of(n * NB, NB), NB)], dec_v.at[n], in_sem.at[1 + NK + n]
        )

    for k in range(NK):
        enc_copy(k).start()
    for n in range(NN):
        dec_copy(n).start()

    barrier = pltpu.get_barrier_semaphore()
    pl.semaphore_signal(barrier, inc=1, device_id=partner, device_id_type=MESH)
    for o in range(1, Z):
        pl.semaphore_signal(barrier, inc=1, device_id=zdev(o), device_id_type=MESH)
    for o in range(1, NL):
        pl.semaphore_signal(barrier, inc=1, device_id=(w, lat_to(o)), device_id_type=MESH)

    def a1(h, k):
        return rc(stA.at[h, k, pc], rxA.at[h, k], a1s.at[h, k], a1r.at[h, k], partner)

    def a2(h, k, o):
        return rc(
            sA.at[h, k, (z + o) % Z], rA.at[h, k, o], a2s.at[h, k, o], a2r.at[h, k, o], zdev(o)
        )

    def own_z(ref, ssem, rsem):
        def send(h, k, o):
            block = ref.at[h, k, c, z]
            return rc(block, block, ssem.at[h, k, o], rsem.at[h, k, o], zdev(o))

        def arrive(h, k, o):
            block = ref.at[h, k, c, (z + Z - o) % Z]
            return rc(block, block, ssem.at[h, k, o], rsem.at[h, k, o], zdev(o))

        return send, arrive

    def own_core(ref, ssem, rsem):
        def send(h, k):
            block = ref.at[h, k, c]
            return rc(block, block, ssem.at[h, k], rsem.at[h, k], partner)

        def arrive(h, k):
            block = ref.at[h, k, pc]
            return rc(block, block, ssem.at[h, k], rsem.at[h, k], partner)

        return send, arrive

    a3, a3in = own_z(acts, a3s, a3r)
    a4, a4in = own_core(acts, a4s, a4r)
    d3, d3in = own_z(dp, d3s, d3r)
    d4, d4in = own_core(dp, d4s, d4r)

    def combine_a(h, k):
        a1(h, k).wait_recv()
        sA[h, k] = stA[h, k, c] + rxA[h, k]
        for o in range(1, Z):
            a2(h, k, o).start()

    c_res.wait()
    pl.semaphore_wait(barrier, 1 + (Z - 1) + (NL - 1))

    def pre_part(h, k):
        p = jnp.dot(res_v[h * TH:(h + 1) * TH, :], enc_v[k], preferred_element_type=F32)
        for j in range(2):
            stA[h, k, j] = p[:, j * KC:(j + 1) * KC].reshape(Z, TB, KC)
        a1(h, k).start()

    def pre_first(k):
        enc_copy(k).wait()
        pre_part(0, k)

        @pl.when(k > 0)
        def _():
            combine_a(0, k - 1)

    loop(NK, pre_first)
    combine_a(0, NK - 1)
    for h in range(1, H):
        loop(NK, lambda k: pre_part(h, k))

    def fwd_a(h, k):
        for o in range(1, Z):
            a3in(h, k, o).wait_recv()
        a4(h, k).start()

    def act_step(h, k):
        for o in range(1, Z):
            a2(h, k, o).wait_recv()
        pre = sA[h, k, z]
        for o in range(1, Z):
            pre = pre + rA[h, k, o]
        pre = pre + bias[k, c]
        preS[h, k] = pre
        acts[h, k, c, z] = jnp.maximum(pre, 0.0).astype(BF16)
        for o in range(1, Z):
            a3(h, k, o).start()

    loop(NK, lambda k: act_step(0, k))
    loop(NK, lambda k: combine_a(1, k))

    def rt_step(n):
        rt_v[n] = res_v[:, pl.ds(pl.multiple_of(n * NB, NB), NB)].T

    loop(NN, rt_step)
    rt_copy = pltpu.make_async_copy(rt_v, rt_o, out_sem.at[0])
    rt_copy.start()

    def b1(h, n, o):
        to = lat_to(o)
        return rc(sB.at[h, n, to], rB.at[h, n, o], bs.at[h, n, o], br.at[h, n, o], (w, to))

    def c1(h, n, o):
        block = err.at[h, n, l]
        return rc(block, block, cs.at[h, n, o], cr.at[h, n, o], (w, lat_to(o)))

    def c1in(h, n, o):
        block = err.at[h, n, lat_from(o)]
        return rc(block, block, cs.at[h, n, o], cr.at[h, n, o], (w, lat_to(o)))

    def rec_step(h, n):
        a = jnp.concatenate(
            [acts[h, k, j].reshape(TH, KC) for k in range(NK) for j in range(2)], axis=1
        )
        r = jnp.dot(a, dec_v[n], preferred_element_type=F32).reshape(NL, TL, NB)
        rf[h, n] = r
        sB[h, n] = r.astype(BF16)
        for o in range(1, NL):
            b1(h, n, o).start()

    def at_step(h, k):
        a = jnp.concatenate([acts[h, k, j].reshape(TH, KC) for j in range(2)], axis=1)
        actsT[h, k] = a.T

    def err_step(h, n):
        for o in range(1, NL):
            b1(h, n, o).wait_recv()
        r = rf[h, n, l]
        for o in range(1, NL):
            r = r + rB[h, n, o].astype(F32)
        own = res_v[
            pl.ds(pl.multiple_of(h * TH + l * TL, TL), TL),
            pl.ds(pl.multiple_of(n * NB, NB), NB),
        ]
        err[h, n, l] = (r + dbias[n] - own.astype(F32)).astype(BF16)
        for o in range(1, NL):
            c1(h, n, o).start()

    def recon(h):
        loop(NK, lambda k: fwd_a(h, k))
        if h == 0:
            for n in range(NN):
                dec_copy(n).wait()
        loop(NK, lambda k: a4in(h, k).wait_recv())
        loop(NN, lambda n: rec_step(h, n))
        loop(NK, lambda k: at_step(h, k))

    recon(0)

    def zero_step(k):
        for s in range(3):
            sacc[s, k] = jnp.zeros(sacc.shape[2:], F32)

    loop(NK, zero_step)

    def err_act(i):
        err_step(0, i)
        act_step(1, i)

    loop(NK, err_act)
    recon(1)

    def dec_rows(n, k):
        return dec_v[n, pl.ds(pl.multiple_of(k * KB, KB), KB), :]

    def dacts_part(h, n, k):
        d = lax.dot_general(
            err[h, n].reshape(TH, NB), dec_rows(n, k), NT, preferred_element_type=F32
        )
        return [d[:, j * KC:(j + 1) * KC].reshape(Z, TB, KC) for j in range(2)]

    def grad_first(n, k):
        grad[n, k] = jnp.dot(
            actsT[0, k], err[0, n].reshape(TH, NB), preferred_element_type=F32
        )

    def grad_last(n, k):
        g = grad[n, k] + jnp.dot(
            actsT[1, k], err[1, n].reshape(TH, NB), preferred_element_type=F32
        )
        grad[n, k] = g
        wt = dec_rows(n, k).astype(F32)
        for s, prod in enumerate((wt * wt, g * wt, g * g)):
            part = prod[:, 0:128]
            for j in range(1, NB // 128):
                part = part + prod[:, j * 128:(j + 1) * 128]
            sacc[s, k] += part

    def err_wait(h, n):
        for o in range(1, NL):
            c1in(h, n, o).wait_recv()

    def d1(h, k):
        return rc(sD.at[h, k, pc], rxD.at[h, k], d1s.at[h, k], d1r.at[h, k], partner)

    def d2(h, k, o):
        return rc(
            sS.at[h, k, (z + o) % Z], rD.at[h, k, o], d2s.at[h, k, o], d2r.at[h, k, o], zdev(o)
        )

    def combine_d(h, k):
        d1(h, k).wait_recv()
        s = dacc[h, k, c] + rxD[h, k].astype(F32)
        dacc[h, k, c] = s
        sS[h, k] = s.astype(BF16)
        for o in range(1, Z):
            d2(h, k, o).start()

    def dacts_add(h, n, k):
        for j, d in enumerate(dacts_part(h, n, k)):
            if isinstance(n, int) and n == 0:
                dacc[h, k, j] = d
            else:
                dacc[h, k, j] += d

    last = NN - 1

    def d_step(h, k):
        for j, d in enumerate(dacts_part(h, last, k)):
            v = dacc[h, k, j] + d
            dacc[h, k, j] = v
            sD[h, k, j] = v.astype(BF16)
        d1(h, k).start()

        @pl.when(k > 0)
        def _():
            combine_d(h, k - 1)

    def dacts(h, beside):
        def step(n):
            err_wait(h, n)

            def k_step(k):
                dacts_add(h, n, k)
                beside(n, k)

            loop(NK, k_step)

        step(0)
        lax.fori_loop(1, last, lambda n, _: (step(n), 0)[1], 0)
        err_wait(h, last)
        loop(NK, lambda k: d_step(h, k))
        combine_d(h, NK - 1)

    def dp_step(h, k):
        for o in range(1, Z):
            d2(h, k, o).wait_recv()
        v = dacc[h, k, c, z]
        for o in range(1, Z):
            v = v + rD[h, k, o].astype(F32)
        dp[h, k, c, z] = jnp.where(preS[h, k] > 0.0, v + PENALTY, 0.0).astype(BF16)
        for o in range(1, Z):
            d3(h, k, o).start()

    def fwd_d(h, k):
        for o in range(1, Z):
            d3in(h, k, o).wait_recv()
        d4(h, k).start()

    dacts(0, lambda n, k: None)

    def err_grad(i):
        err_step(1, i)
        loop(NK, lambda k: grad_first(i, k))

    loop(NN, err_grad)
    loop(NK, lambda k: dp_step(0, k))
    dacts(1, grad_last)

    def gd_step(k):
        grad_last(last, k)
        for s in range(3):
            stv[k, s:s + 1, :] = jnp.sum(sacc[s, k].T, axis=0, keepdims=True)
        stv[k, 3:8, :] = jnp.zeros((5, KB), F32)
        dp_step(1, k)

    loop(NK, gd_step)

    e1 = rc(stv, rst, e1s, e1r, partner)
    e1.start()

    def e2(o):
        return rc(ss, rs2.at[o], e2s.at[o], e2r.at[o], zdev(o))

    loop(NK, lambda k: fwd_d(0, k))
    e1.wait_recv()
    ss[...] = stv[...] + rst[...]
    for o in range(1, Z):
        e2(o).start()

    loop(NK, lambda k: fwd_d(1, k))
    for o in range(1, Z):
        e2(o).wait_recv()

    def nd_copy(k):
        return pltpu.make_async_copy(
            nd_v.at[k], nd_o.at[pl.ds(pl.multiple_of(k * KB, KB), KB), :], out_sem.at[2 + k]
        )

    def nd_step(k):
        t = ss[k]
        for o in range(1, Z):
            t = t + rs2[o, k]
        ww, gw, gg = t[0:1], t[1:2], t[2:3]
        coef = gw / (ww + EPS)
        sq = (
            ww
            - 2.0 * STEP * (gw - coef * ww)
            + STEP * STEP * (gg - 2.0 * coef * gw + coef * coef * ww)
        )
        inv = 1.0 / jnp.sqrt(sq + EPS)
        up = jnp.broadcast_to((1.0 + STEP * coef) * inv, (128, KB)).T
        down = jnp.broadcast_to(STEP * inv, (128, KB)).T
        for n in range(NN):
            for j in range(NB // 128):
                wt = dec_v[n, pl.ds(pl.multiple_of(k * KB, KB), KB), j * 128:(j + 1) * 128]
                g = grad[n, k, :, j * 128:(j + 1) * 128]
                first = n * NB + j * 128
                nd_v[k, :, first:first + 128] = (wt.astype(F32) * up - g * down).astype(BF16)
        nd_copy(k).start()

    loop(NK, nd_step)
    for h in range(H):
        loop(NK, lambda k: d4in(h, k).wait_recv())
    dp_copy = pltpu.make_async_copy(dp, dp_o, out_sem.at[1])
    dp_copy.start()

    def drain(k):
        for h in range(H):
            for first in (a1, a4, d1, d4):
                first(h, k).wait_send()
            for o in range(1, Z):
                for each in (a2, a3, d2, d3):
                    each(h, k, o).wait_send()
        nd_copy(k).wait()

    def drain_n(n):
        for h in range(H):
            for o in range(1, NL):
                b1(h, n, o).wait_send()
                c1(h, n, o).wait_send()

    loop(NK, drain)
    loop(NN, drain_n)
    e1.wait_send()
    for o in range(1, Z):
        e2(o).wait_send()
    rt_copy.wait()
    dp_copy.wait()


def enc_grad_kernel(rt, dp, out):
    halves, blocks = dp.shape[:2]
    d = jnp.concatenate(
        [
            jnp.concatenate([dp[h, k] for k in range(blocks)], axis=1)
            for h in range(halves)
        ],
        axis=0,
    )
    out[...] = jnp.dot(rt[0], d, preferred_element_type=F32).astype(BF16)


def fused(W, NL, residuals, encoder, enc_bias, decoder, dec_bias):
    T, DW = residuals.shape
    LL = encoder.shape[1]
    Z = W // 2
    NK, NN = 4, 4
    KB, NB = LL // NK, DW // NN
    H = 2
    TH = T // H
    TB, TL = TH // Z, TH // NL
    KC = KB // 2
    V = pltpu.VMEM
    dma = pltpu.SemaphoreType.DMA
    sums, part, rows = (H, NK, 2, Z, TB, KC), (H, NK, Z, TB, KC), (H, NN, NL, TL, NB)
    one, per_z, per_l = (H, NK), (H, NK, Z), (H, NN, NL)
    scratch = [
        V((T, DW), BF16), V((NK, DW, KB), BF16), V((NN, LL, NB), BF16),
        V(sums, F32), V(part, F32), V(part, F32), V(part, F32), V((H, NK, TB, KC), F32),
        V(sums, BF16), V((H, NK, KB, TH), BF16), V((NN, NB, T), BF16),
        V(rows, F32), V(rows, BF16), V(rows, BF16), V(rows, BF16),
        V(sums, F32), V(sums, BF16), V(part, BF16), V(part, BF16), V(part, BF16), V(sums, BF16),
        V((NN, NK, KB, NB), F32), V((3, NK, KB, 128), F32),
        V((NK, 8, KB), F32), V((NK, 8, KB), F32), V((NK, 8, KB), F32), V((Z, NK, 8, KB), F32),
        V((NK, KB, DW), BF16),
        dma((1 + NK + NN,)), dma((2 + NK,)),
        dma(one), dma(one), dma(per_z), dma(per_z), dma(per_z), dma(per_z), dma(one), dma(one),
        dma(per_l), dma(per_l), dma(per_l), dma(per_l),
        dma(one), dma(one), dma(per_z), dma(per_z), dma(per_z), dma(per_z), dma(one), dma(one),
        dma, dma, dma((Z,)), dma((Z,)),
    ]
    hbm = pl.BlockSpec(memory_space=pl.ANY)
    vm = pl.BlockSpec(memory_space=pltpu.VMEM)
    new_decoder, dp, rt = pl.pallas_call(
        functools.partial(step_kernel, Z, NL, NK, NN),
        out_shape=(
            jax.ShapeDtypeStruct((LL, DW), BF16),
            jax.ShapeDtypeStruct(sums, BF16),
            jax.ShapeDtypeStruct((NN, NB, T), BF16),
        ),
        in_specs=[hbm, hbm, vm, hbm, vm],
        out_specs=(hbm, hbm, hbm),
        scratch_shapes=scratch,
        compiler_params=pltpu.CompilerParams(
            collective_id=0, has_side_effects=True, vmem_limit_bytes=60 * 2**20
        ),
        name="sae_step",
    )(residuals, encoder, enc_bias.reshape(NK, 2, 1, KC), decoder, dec_bias.reshape(NN, 1, NB))
    enc_grad = pl.pallas_call(
        enc_grad_kernel,
        grid=(NN,),
        out_shape=jax.ShapeDtypeStruct((DW, LL), BF16),
        in_specs=[
            pl.BlockSpec((1, NB, T), lambda i: (i, 0, 0)),
            pl.BlockSpec((H, 2 * NK, TH, KC), lambda i: (0, 0, 0, 0)),
        ],
        out_specs=pl.BlockSpec((NB, LL), lambda i: (i, 0)),
        compiler_params=pltpu.CompilerParams(vmem_limit_bytes=60 * 2**20),
        cost_estimate=pl.CostEstimate(
            flops=2 * T * DW * LL, bytes_accessed=2 * (T * DW + T * LL + DW * LL),
            transcendentals=0,
        ),
        name="enc_grad",
    )(rt, dp.reshape(H, 2 * NK, TH, KC))
    return enc_grad, new_decoder


def plain(residuals, encoder, enc_bias, decoder, dec_bias):
    tokens = residuals.shape[0]
    lat_count = lax.axis_size("lat")
    lat_rows = tokens // lat_count
    rows = residuals
    pre_rows = (
        lax.psum_scatter(
            jnp.dot(rows, encoder, preferred_element_type=jnp.float32),
            "width",
            scatter_dimension=0,
            tiled=True,
        )
        + enc_bias
    )
    active_rows = pre_rows > 0.0
    act_rows = jnp.maximum(pre_rows, 0.0).astype(jnp.bfloat16)
    acts = lax.all_gather(act_rows, "width", axis=0, tiled=True)
    rows = acts
    recon_rows = lax.psum_scatter(
        jnp.dot(rows, decoder, preferred_element_type=jnp.float32),
        "lat",
        scatter_dimension=0,
        tiled=True,
    )
    first = lax.axis_index("lat") * lat_rows
    own_rows = lax.dynamic_slice_in_dim(residuals, first, lat_rows, 0)
    error_part = (recon_rows + dec_bias - own_rows.astype(jnp.float32)).astype(jnp.bfloat16)
    error = lax.all_gather(error_part, "lat", axis=0, tiled=True)
    rows = error
    dacts_rows = (
        lax.psum_scatter(
            lax.dot_general(
                rows, decoder, (((1,), (1,)), ((), ())), preferred_element_type=jnp.float32
            ),
            "width",
            scatter_dimension=0,
            tiled=True,
        )
        + PENALTY
    )
    dpre_part = jnp.where(active_rows, dacts_rows, 0.0).astype(jnp.bfloat16)
    dpre = lax.all_gather(dpre_part, "width", axis=0, tiled=True)
    enc_grad = lax.dot_general(
        residuals, dpre, (((0,), (0,)), ((), ())), preferred_element_type=jnp.float32
    ).astype(jnp.bfloat16)
    grad = lax.dot_general(
        acts, error, (((0,), (0,)), ((), ())), preferred_element_type=jnp.float32
    )
    weight = decoder.astype(jnp.float32)
    ww, gw, gg = lax.psum(
        (
            jnp.sum(weight * weight, axis=1),
            jnp.sum(grad * weight, axis=1),
            jnp.sum(grad * grad, axis=1),
        ),
        "width",
    )
    coef_row = gw / (ww + EPS)
    coef = coef_row[:, None]
    moved = weight - STEP * (grad - coef * weight)
    squared = (
        ww
        - 2.0 * STEP * (gw - coef_row * ww)
        + STEP * STEP * (gg - 2.0 * coef_row * gw + coef_row * coef_row * ww)
    )
    new_decoder = (moved / jnp.sqrt(squared + EPS)[:, None]).astype(jnp.bfloat16)
    return (enc_grad, new_decoder)


def per_device(W, NL, residuals, encoder, enc_bias, decoder, dec_bias):
    T, DW = residuals.shape
    LL = encoder.shape[1]
    args = (residuals, encoder, enc_bias, decoder, dec_bias)
    fits = W % 2 == 0 and NL % 2 == 0 and T % (16 * W) == 0 and T % (32 * NL) == 0
    if fits and DW % 512 == 0 and LL % 1024 == 0 and T % 128 == 0:
        return fused(W, NL, *args)
    return plain(*args)


def solution(mesh):
    return jax.shard_map(
        functools.partial(per_device, mesh.shape["width"], mesh.shape["lat"]),
        mesh=mesh,
        in_specs=(P(None, "width"), P("width", "lat"), P("lat"), P("lat", "width"), P("width")),
        out_specs=(P("width", "lat"), P("lat", "width")),
        check_vma=False,
    )
```

time: 111 us -> 94 us (0.85)
  Pallas kernels: 106 us -> 88.3 us
    pallas_call x1, Pallas kernels: 102 us -> 82.5 us  [fused(): pl.pallas_call(functools.partial(step_kernel, Z, NL, NK, NN), out_shape=(...]
    pallas_call x1, Pallas kernels: 4.08 us -> 5.79 us  [fused(): pl.pallas_call(enc_grad_kernel, grid=(NN,), out_shape=jax.ShapeDtypeStruc...]
    unnamed x7 -> x1, local copies, waits for them, and re-layouts: 4.55 us -> 4.79 us
where the time goes in v2:
time: 94 us; the launch traced here: 93.8 us
  Pallas kernels  88.3 us (94%)
  local copies, waits for them, and re-layouts  4.79 us (5%)
    pallas_call x1, Pallas kernels, fused(): pl.pallas_call(functools.partial(step_kernel, Z, NL, NK, NN), out_shape=(...  82.5 us
    pallas_call x1, Pallas kernels, fused(): pl.pallas_call(enc_grad_kernel, grid=(NN,), out_shape=jax.ShapeDtypeStruc...  5.79 us
    unnamed x1, local copies, waits for them, and re-layouts  4.79 us

profile of v2, /device:TPU:0, one launch (start us, length us, event | category | flops | bytes accessed | tf_op | source)
XLA Modules:
  0.0 93.8 jit_solution(4598186714890756634)
XLA Ops:
  0.6 82.5 %sae_step.1 = (bf16[1024,2048]{1,0:T(8,128)(2,1)}, bf16[2,4,2,4,48,128]{5,4,3,2,1,0:T(8,128)(2,1)}, bf16[4,512,384]{2,1,0:T(8,128)(2,1)}) custom-call(bf16[384,2048]{1,0:T(8,128)(2,1)} %res_h.1, bf16[2048,1024]{1,0:T(8,128)(2,1)} %enc_h.1, f32[4,2,1,128]{3,2,1,0:T(1,128)} %bitcast.5, bf16[1024,2048]{1,0:T(8,128)(2,1)} %dec_h.1, f32[4,1,512]{2,1,0:T(1,128)} %bitcast.4), custom_call_target="tpu_custom_call" | custom-call | tf_op jit(solution)/shard_map/sae_step/pallas_call | solution.py:471
  83.2 5.8 %enc_grad.1 = bf16[2048,1024]{1,0:T(8,128)(2,1)} custom-call(bf16[4,512,384]{2,1,0:T(8,128)(2,1)} %get-tuple-element.5.rt, bf16[2,8,192,128]{3,2,1,0:T(8,128)(2,1)} %bitcast.3), custom_call_target="tpu_custom_call" | custom-call | flops 1610612736 | bytes 6553600 | tf_op jit(solution)/shard_map/enc_grad/pallas_call | solution.py:486
  89.0 4.8 %copy.8 = bf16[1024,2048]{1,0:T(8,128)(2,1)} copy(bf16[1024,2048]{1,0:T(8,128)(2,1)} %get-tuple-element.11) | data formatting | bytes 8388608

commit v3 on v2

--- a/solution.py
+++ b/solution.py
@@ -20,7 +20,7 @@
     res_h, enc_h, bias, dec_h, dbias,
     nd_o, dp_o, rt_o,
     res_v, enc_v, dec_v, stA, rxA, sA, rA, preS, acts, actsT, rt_v,
-    rf, sB, rB, err, dacc, sD, rxD, sS, rD, dp, grad, sacc, stv, rst, ss, rs2, nd_v,
+    rf, sB, sB2, rB, err, dacc, sD, rxD, sS, rD, dp, grad, sacc, stv, rst, ss, rs2, nd_v,
     in_sem, out_sem,
     a1s, a1r, a2s, a2r, a3s, a3r, a4s, a4r,
     bs, br, cs, cr,
@@ -45,8 +45,16 @@
     def lat_to(o):
         return ((l // 2 + o // 2) % (NL // 2)) * 2 + (l % 2 + o % 2) % 2
 
-    def lat_from(o):
-        return ((l // 2 + NL // 2 - o // 2) % (NL // 2)) * 2 + (l % 2 + o % 2) % 2
+    ly, lx = l // 2, l % 2
+    diag = (1 - ly) * 2 + 1 - lx
+
+    def first_of(n):
+        q = (n + c) % 2
+        return (ly + q) % 2 * 2 + (lx + 1 - q) % 2
+
+    def second_of(n):
+        q = (n + c) % 2
+        return (ly + 1 - q) % 2 * 2 + (lx + q) % 2
 
     def rc(src, dst, ssem, rsem, dev):
         return pltpu.make_async_remote_copy(
@@ -173,16 +181,38 @@
     rt_copy.start()
 
     def b1(h, n, o):
-        to = lat_to(o)
-        return rc(sB.at[h, n, to], rB.at[h, n, o], bs.at[h, n, o], br.at[h, n, o], (w, to))
-
-    def c1(h, n, o):
-        block = err.at[h, n, l]
-        return rc(block, block, cs.at[h, n, o], cr.at[h, n, o], (w, lat_to(o)))
-
-    def c1in(h, n, o):
-        block = err.at[h, n, lat_from(o)]
-        return rc(block, block, cs.at[h, n, o], cr.at[h, n, o], (w, lat_to(o)))
+        to = first_of(n)
+        return rc(
+            sB.at[h, n, to if o == 0 else diag], rB.at[h, n, o],
+            bs.at[h, n, o], br.at[h, n, o], (w, to),
+        )
+
+    def b2(h, n):
+        return rc(
+            sB2.at[h, n], rB.at[h, n, 2], bs.at[h, n, 2], br.at[h, n, 2], (w, second_of(n))
+        )
+
+    def c_copy(h, n, o, block, to):
+        ref = err.at[h, n, block]
+        return rc(ref, ref, cs.at[h, n, o], cr.at[h, n, o], (w, to))
+
+    def c1(h, n):
+        return c_copy(h, n, 0, l, second_of(n))
+
+    def c1in(h, n):
+        return c_copy(h, n, 0, second_of(n), second_of(n))
+
+    def c2(h, n):
+        return c_copy(h, n, 1, l, first_of(n))
+
+    def c2in(h, n):
+        return c_copy(h, n, 1, first_of(n), first_of(n))
+
+    def c3(h, n):
+        return c_copy(h, n, 2, second_of(n), first_of(n))
+
+    def c3in(h, n):
+        return c_copy(h, n, 2, diag, first_of(n))
 
     def rec_step(h, n):
         a = jnp.concatenate(
@@ -191,26 +221,33 @@
         r = jnp.dot(a, dec_v[n], preferred_element_type=F32).reshape(NL, TL, NB)
         rf[h, n] = r
         sB[h, n] = r.astype(BF16)
-        for o in range(1, NL):
-            b1(h, n, o).start()
+        b1(h, n, 1).start()
+        b1(h, n, 0).start()
+
+    def mid_step(h, n):
+        b1(h, n, 1).wait_recv()
+        sB2[h, n] = (rf[h, n, second_of(n)] + rB[h, n, 1].astype(F32)).astype(BF16)
+        b2(h, n).start()
 
     def at_step(h, k):
         a = jnp.concatenate([acts[h, k, j].reshape(TH, KC) for j in range(2)], axis=1)
         actsT[h, k] = a.T
 
     def err_step(h, n):
-        for o in range(1, NL):
-            b1(h, n, o).wait_recv()
-        r = rf[h, n, l]
-        for o in range(1, NL):
-            r = r + rB[h, n, o].astype(F32)
+        b1(h, n, 0).wait_recv()
+        b2(h, n).wait_recv()
+        r = rf[h, n, l] + rB[h, n, 0].astype(F32) + rB[h, n, 2].astype(F32)
         own = res_v[
             pl.ds(pl.multiple_of(h * TH + l * TL, TL), TL),
             pl.ds(pl.multiple_of(n * NB, NB), NB),
         ]
         err[h, n, l] = (r + dbias[n] - own.astype(F32)).astype(BF16)
-        for o in range(1, NL):
-            c1(h, n, o).start()
+        c1(h, n).start()
+        c2(h, n).start()
+
+    def fwd_err(h, n):
+        c1in(h, n).wait_recv()
+        c3(h, n).start()
 
     def recon(h):
         loop(NK, lambda k: fwd_a(h, k))
@@ -229,11 +266,18 @@
 
     loop(NK, zero_step)
 
+    loop(NN, lambda n: mid_step(0, n))
+
     def err_act(i):
         err_step(0, i)
         act_step(1, i)
 
+        @pl.when(i > 0)
+        def _():
+            fwd_err(0, i - 1)
+
     loop(NK, err_act)
+    fwd_err(0, NN - 1)
     recon(1)
 
     def dec_rows(n, k):
@@ -263,8 +307,8 @@
             sacc[s, k] += part
 
     def err_wait(h, n):
-        for o in range(1, NL):
-            c1in(h, n, o).wait_recv()
+        c2in(h, n).wait_recv()
+        c3in(h, n).wait_recv()
 
     def d1(h, k):
         return rc(sD.at[h, k, pc], rxD.at[h, k], d1s.at[h, k], d1r.at[h, k], partner)
@@ -302,7 +346,7 @@
         def _():
             combine_d(h, k - 1)
 
-    def dacts(h, beside):
+    def dacts(h, beside, after):
         def step(n):
             err_wait(h, n)
 
@@ -311,12 +355,14 @@
                 beside(n, k)
 
             loop(NK, k_step)
+            after(n)
 
         step(0)
         lax.fori_loop(1, last, lambda n, _: (step(n), 0)[1], 0)
         err_wait(h, last)
         loop(NK, lambda k: d_step(h, k))
         combine_d(h, NK - 1)
+        after(last)
 
     def dp_step(h, k):
         for o in range(1, Z):
@@ -333,15 +379,20 @@
             d3in(h, k, o).wait_recv()
         d4(h, k).start()
 
-    dacts(0, lambda n, k: None)
+    dacts(0, lambda n, k: None, lambda n: mid_step(1, n))
 
     def err_grad(i):
         err_step(1, i)
         loop(NK, lambda k: grad_first(i, k))
 
+        @pl.when(i > 0)
+        def _():
+            fwd_err(1, i - 1)
+
     loop(NN, err_grad)
+    fwd_err(1, NN - 1)
     loop(NK, lambda k: dp_step(0, k))
-    dacts(1, grad_last)
+    dacts(1, grad_last, lambda n: None)
 
     def gd_step(k):
         grad_last(last, k)
@@ -412,9 +463,10 @@
 
     def drain_n(n):
         for h in range(H):
-            for o in range(1, NL):
+            for o in range(2):
                 b1(h, n, o).wait_send()
-                c1(h, n, o).wait_send()
+            for each in (b2, c1, c2, c3):
+                each(h, n).wait_send()
 
     loop(NK, drain)
     loop(NN, drain_n)
@@ -425,7 +477,8 @@
     dp_copy.wait()
 
 
-def enc_grad_kernel(rt, dp, out):
+def enc_grad_kernel(rt, dp, nd, out, nd_out):
+    nd_out[...] = nd[...]
     halves, blocks = dp.shape[:2]
     d = jnp.concatenate(
         [
@@ -450,12 +503,12 @@
     V = pltpu.VMEM
     dma = pltpu.SemaphoreType.DMA
     sums, part, rows = (H, NK, 2, Z, TB, KC), (H, NK, Z, TB, KC), (H, NN, NL, TL, NB)
-    one, per_z, per_l = (H, NK), (H, NK, Z), (H, NN, NL)
+    one, per_z, per_l = (H, NK), (H, NK, Z), (H, NN, 3)
     scratch = [
         V((T, DW), BF16), V((NK, DW, KB), BF16), V((NN, LL, NB), BF16),
         V(sums, F32), V(part, F32), V(part, F32), V(part, F32), V((H, NK, TB, KC), F32),
         V(sums, BF16), V((H, NK, KB, TH), BF16), V((NN, NB, T), BF16),
-        V(rows, F32), V(rows, BF16), V(rows, BF16), V(rows, BF16),
+        V(rows, F32), V(rows, BF16), V((H, NN, TL, NB), BF16), V((H, NN, 3, TL, NB), BF16), V(rows, BF16),
         V(sums, F32), V(sums, BF16), V(part, BF16), V(part, BF16), V(part, BF16), V(sums, BF16),
         V((NN, NK, KB, NB), F32), V((3, NK, KB, 128), F32),
         V((NK, 8, KB), F32), V((NK, 8, KB), F32), V((NK, 8, KB), F32), V((Z, NK, 8, KB), F32),
@@ -483,22 +536,29 @@
         ),
         name="sae_step",
     )(residuals, encoder, enc_bias.reshape(NK, 2, 1, KC), decoder, dec_bias.reshape(NN, 1, NB))
-    enc_grad = pl.pallas_call(
+    enc_grad, new_decoder = pl.pallas_call(
         enc_grad_kernel,
-        grid=(NN,),
-        out_shape=jax.ShapeDtypeStruct((DW, LL), BF16),
+        grid=(2 * NN,),
+        out_shape=(
+            jax.ShapeDtypeStruct((DW, LL), BF16),
+            jax.ShapeDtypeStruct((LL, DW), BF16),
+        ),
         in_specs=[
-            pl.BlockSpec((1, NB, T), lambda i: (i, 0, 0)),
+            pl.BlockSpec((1, NB // 2, T), lambda i: (i // 2, i % 2, 0)),
             pl.BlockSpec((H, 2 * NK, TH, KC), lambda i: (0, 0, 0, 0)),
+            pl.BlockSpec((LL // (2 * NN), DW), lambda i: (i, 0)),
         ],
-        out_specs=pl.BlockSpec((NB, LL), lambda i: (i, 0)),
+        out_specs=(
+            pl.BlockSpec((NB // 2, LL), lambda i: (i, 0)),
+            pl.BlockSpec((LL // (2 * NN), DW), lambda i: (i, 0)),
+        ),
         compiler_params=pltpu.CompilerParams(vmem_limit_bytes=60 * 2**20),
         cost_estimate=pl.CostEstimate(
-            flops=2 * T * DW * LL, bytes_accessed=2 * (T * DW + T * LL + DW * LL),
+            flops=2 * T * DW * LL, bytes_accessed=2 * (T * DW + T * LL + 3 * DW * LL),
             transcendentals=0,
         ),
         name="enc_grad",
-    )(rt, dp.reshape(H, 2 * NK, TH, KC))
+    )(rt, dp.reshape(H, 2 * NK, TH, KC), new_decoder)
     return enc_grad, new_decoder
 
 
@@ -575,7 +635,7 @@
     T, DW = residuals.shape
     LL = encoder.shape[1]
     args = (residuals, encoder, enc_bias, decoder, dec_bias)
-    fits = W % 2 == 0 and NL % 2 == 0 and T % (16 * W) == 0 and T % (32 * NL) == 0
+    fits = W % 2 == 0 and NL == 4 and T % (16 * W) == 0 and T % (32 * NL) == 0
     if fits and DW % 512 == 0 and LL % 1024 == 0 and T % 128 == 0:
         return fused(W, NL, *args)
     return plain(*args)

time: 94 us -> 94.3 us (level)
  Pallas kernels: 88.3 us -> 93.4 us
  local copies, waits for them, and re-layouts: 4.79 us -> 0 us
    unnamed x1 -> x0, local copies, waits for them, and re-layouts: 4.79 us -> none
    pallas_call x1, Pallas kernels: 5.79 us -> 9.97 us  [fused(): pl.pallas_call(enc_grad_kernel, grid=(2 * NN,), out_shape=(jax.ShapeDtype...]
where the time goes in v3:
time: 94.3 us; the launch traced here: 94 us
  Pallas kernels  93.4 us (99%)
    pallas_call x1, Pallas kernels, fused(): pl.pallas_call(functools.partial(step_kernel, Z, NL, NK, NN), out_shape=(...  83.4 us
    pallas_call x1, Pallas kernels, fused(): pl.pallas_call(enc_grad_kernel, grid=(2 * NN,), out_shape=(jax.ShapeDtype...  9.97 us

profile of v3, /device:TPU:0, one launch (start us, length us, event | category | flops | bytes accessed | tf_op | source)
XLA Modules:
  0.0 94.0 jit_solution(13385870949473746811)
XLA Ops:
  0.6 83.4 %sae_step.1 = (bf16[1024,2048]{1,0:T(8,128)(2,1)}, bf16[2,4,2,4,48,128]{5,4,3,2,1,0:T(8,128)(2,1)}, bf16[4,512,384]{2,1,0:T(8,128)(2,1)}) custom-call(bf16[384,2048]{1,0:T(8,128)(2,1)} %res_h.1, bf16[2048,1024]{1,0:T(8,128)(2,1)} %enc_h.1, f32[4,2,1,128]{3,2,1,0:T(1,128)} %bitcast.5, bf16[1024,2048]{1,0:T(8,128)(2,1)} %dec_h.1, f32[4,1,512]{2,1,0:T(1,128)} %bitcast.4), custom_call_target="tpu_custom_call" | custom-call | tf_op jit(solution)/shard_map/sae_step/pallas_call | solution.py:524
  84.0 10.0 %enc_grad.1 = (bf16[2048,1024]{1,0:T(8,128)(2,1)}, bf16[1024,2048]{1,0:T(8,128)(2,1)}) custom-call(bf16[4,512,384]{2,1,0:T(8,128)(2,1)} %get-tuple-element.5.rt, bf16[2,8,192,128]{3,2,1,0:T(8,128)(2,1)} %bitcast.3, bf16[1024,2048]{1,0:T(8,128)(2,1)} %get-tuple-element.7.nd), custom_call_target="tpu_custom_call" | custom-call | flops 1610612736 | bytes 14942208 | tf_op jit(solution)/shard_map/enc_grad/pallas_call | solution.py:539
